TPU v7x, 32 devices: a whole 2x2x4 slice. The times are simulated.
32 devices in a mesh: brick: 16 (over z, y, core), chan: 2 (over x).
Axes of the slice: x: 2, y: 2, z: 4, core: 2. Of those that a mesh axis runs over, the one named last changes fastest.
Arguments:
- volume: bfloat16 [32, 16, 64, 256], P('brick', 'chan'), may hold values from -6 to 6
- first_weight: bfloat16 [3, 3, 3, 256, 256], replicated, may hold values from -0.078125 to 0.078125
- second_weight: bfloat16 [3, 3, 3, 256, 256], replicated, may hold values from -0.078125 to 0.078125
- coarse_weight: bfloat16 [3, 3, 3, 256, 512], P(None, None, None, None, 'chan'), may hold values from -0.078125 to 0.078125
- projection: bfloat16 [512, 256], P('chan'), may hold values from -0.25 to 0.25
Outputs:
- merged: bfloat16 [32, 16, 64, 256], P('brick', 'chan')
All inputs are finite; a program needn't handle non-finite values.
Results may differ from a plain program's by a relative error of at most 0.011.
Values may be sent and summed in bfloat16 or wider, within the bound.
No kernel may reach another device: no remote copies, remote signals or barrier semaphores. Data moves between devices by JAX's collectives and lax.ppermute only.
A program may use at most 64 MiB of HBM per device.

v0:
```python
import jax
import jax.numpy as jnp
from jax import lax
from jax.sharding import PartitionSpec as P


def extended(block, sides, width):
    for axis, dim in sides:
        count = lax.axis_size(axis)
        forward = [(i, i + 1) for i in range(count - 1)]
        backward = [(target, source) for source, target in forward]
        low = lax.ppermute(
            lax.slice_in_dim(block, block.shape[dim] - width, None, axis=dim), axis, forward
        )
        high = lax.ppermute(lax.slice_in_dim(block, 0, width, axis=dim), axis, backward)
        block = jnp.concatenate([low, block, high], axis=dim)
    return block


def convolve(padded, weight):
    rows_x = padded.shape[0] - 2
    rows_y = padded.shape[1] - 2
    rows_z = padded.shape[2] - 2
    inputs_count = padded.shape[3]
    outputs_count = weight.shape[4]
    total = jnp.zeros((rows_x * rows_y * rows_z, outputs_count), jnp.float32)
    for offset_x in range(3):
        for offset_y in range(3):
            for offset_z in range(3):
                window = padded[
                    offset_x : offset_x + rows_x,
                    offset_y : offset_y + rows_y,
                    offset_z : offset_z + rows_z,
                ]
                window = window.reshape(-1, inputs_count)
                total = total + jnp.dot(
                    window, weight[offset_x, offset_y, offset_z], preferred_element_type=jnp.float32
                )
    return total.reshape(rows_x, rows_y, rows_z, outputs_count)


def fine_layer(field, weight):
    padded = extended(field, (("brick", 0), ("chan", 1)), 1)
    padded = jnp.pad(padded, ((0, 0), (0, 0), (1, 1), (0, 0)))
    return jnp.maximum(convolve(padded, weight), 0.0).astype(jnp.bfloat16)


def shards(volume, first_weight, second_weight, coarse_weight, projection):
    layer_one = fine_layer(volume, first_weight)
    skipped = fine_layer(layer_one, second_weight)
    size_x, size_y, size_z, channels_in = skipped.shape
    blocks = skipped.astype(jnp.float32).reshape(
        size_x // 2, 2, size_y // 2, 2, size_z // 2, 2, channels_in
    )
    pooled = jnp.mean(blocks, axis=(1, 3, 5)).astype(jnp.bfloat16)
    brick_cells = lax.all_gather(pooled, "chan", axis=1, tiled=True)
    padded = extended(brick_cells, (("brick", 0),), 1)
    padded = jnp.pad(padded, ((0, 0), (1, 1), (1, 1), (0, 0)))
    coarse = jnp.maximum(convolve(padded, coarse_weight), 0.0).astype(jnp.bfloat16)
    own_cells = lax.all_to_all(coarse, "chan", split_axis=1, concat_axis=3, tiled=True)
    whole_projection = lax.all_gather(projection, "chan", axis=0, tiled=True)
    own_shape = own_cells.shape
    lifted = jnp.dot(
        own_cells.reshape(-1, own_shape[3]), whole_projection, preferred_element_type=jnp.float32
    )
    lifted = lifted.reshape(own_shape[0], own_shape[1], own_shape[2], channels_in)
    upsampled = jnp.repeat(jnp.repeat(jnp.repeat(lifted, 2, axis=0), 2, axis=1), 2, axis=2)
    return (skipped.astype(jnp.float32) + upsampled).astype(jnp.bfloat16)


def solution(mesh):
    in_specs = (
        P("brick", "chan", None, None),
        P(),
        P(),
        P(None, None, None, None, "chan"),
        P("chan", None),
    )
    out_specs = P("brick", "chan", None, None)
    return jax.shard_map(shards, mesh=mesh, in_specs=in_specs, out_specs=out_specs, check_vma=False)
```

profile of v0, /device:TPU:21, one launch (start us, length us, event | category | flops | bytes accessed | tf_op | source)
XLA Modules:
  0.0 105.2 jit_solution(181432394441561462)
XLA Ops:
  0.0 1.2 %fusion.277 = (bf16[1,8,64,256]{3,2,1,0:T(8,128)(2,1)S(1)}, bf16[1,8,64,256]{3,2,1,0:T(8,128)(2,1)S(1)}) fusion(bf16[2,8,64,256]{3,2,1,0:T(8,128)(2,1)} %param.5), kind=kLoop, calls=%fused_computation.343 | loop fusion | bytes 1048576 | tf_op jit(solution)/shard_map/slice | solution.py:15
  1.2 3.8 %collective-permute-start = (bf16[1,8,64,256]{3,2,1,0:T(8,128)(2,1)S(1)}, bf16[1,8,64,256]{3,2,1,0:T(8,128)(2,1)S(1)}, u32[]{:S(2)}, u32[]{:S(2)}) collective-permute-start(bf16[1,8,64,256]{3,2,1,0:T(8,128)(2,1)S(1)} %get-tuple-element.94), channel_id=1, source_target_pairs={{0,2},{2,4},{4,6},{6,8},{8,10},{10,12},{12,14},{14,16},{16,18},{18... | collective-permute-start | bytes 786440 | tf_op jit(solution)/shard_map/ppermute | solution.py:12
  5.1 1.9 %collective-permute-start.1 = (bf16[1,8,64,256]{3,2,1,0:T(8,128)(2,1)S(1)}, bf16[1,8,64,256]{3,2,1,0:T(8,128)(2,1)S(1)}, u32[]{:S(2)}, u32[]{:S(2)}) collective-permute-start(bf16[1,8,64,256]{3,2,1,0:T(8,128)(2,1)S(1)} %get-tuple-element.93), channel_id=1, source_target_pairs={{2,0},{4,2},{6,4},{8,6},{10,8},{12,10},{14,12},{16,14},{18,16},{20... | collective-permute-start | bytes 786440 | tf_op jit(solution)/shard_map/ppermute | solution.py:15
  7.0 1.4 %fusion.160 = f32[1024,256]{1,0:T(8,128)S(1)} fusion(bf16[1024,256]{1,0:T(8,128)(2,1)} %bitcast.426, bf16[3,3,3,256,256]{4,3,2,1,0:T(8,128)(2,1)} %param.6), kind=kOutput, calls=%fused_computation.221 | convolution fusion | flops 134217728 | bytes 1703936 | tf_op jit(solution)/shard_map/dot_general | solution.py:36
  8.4 5.3 %collective-permute-done.1 = bf16[1,8,64,256]{3,2,1,0:T(8,128)(2,1)S(1)} collective-permute-done((bf16[1,8,64,256]{3,2,1,0:T(8,128)(2,1)S(1)}, bf16[1,8,64,256]{3,2,1,0:T(8,128)(2,1)S(1)}, u32[]{:S(2)}, u32[]{:S(2)}) %collective-permute-start.1) | collective-permute-done | bytes 262176 | tf_op jit(solution)/shard_map/ppermute | solution.py:15
  13.9 3.1 %collective-permute-start.2 = (bf16[4,1,64,256]{3,2,1,0:T(8,128)(2,1)S(1)}, bf16[4,1,64,256]{3,2,1,0:T(8,128)(2,1)S(1)}, u32[]{:S(2)}, u32[]{:S(2)}) collective-permute-start(bf16[4,1,64,256]{3,2,1,0:T(8,128)(2,1)S(1)} %get-tuple-element.60), channel_id=1, source_target_pairs={{0,1},{2,3},{4,5},{6,7},{8,9},{10,11},{12,13},{14,15},{16,17},{18,... | collective-permute-start | bytes 393224 | tf_op jit(solution)/shard_map/ppermute | solution.py:12
  17.0 1.3 %collective-permute-start.3 = (bf16[4,1,64,256]{3,2,1,0:T(8,128)(2,1)S(1)}, bf16[4,1,64,256]{3,2,1,0:T(8,128)(2,1)S(1)}, u32[]{:S(2)}, u32[]{:S(2)}) collective-permute-start(bf16[4,1,64,256]{3,2,1,0:T(8,128)(2,1)S(1)} %get-tuple-element.61), channel_id=1, source_target_pairs={{1,0},{3,2},{5,4},{7,6},{9,8},{11,10},{13,12},{15,14},{17,16},{19,... | collective-permute-start | bytes 393224 | tf_op jit(solution)/shard_map/ppermute | solution.py:15
  19.0 3.8 %collective-permute-done.3 = bf16[4,1,64,256]{3,2,1,0:T(8,128)(2,1)S(1)} collective-permute-done((bf16[4,1,64,256]{3,2,1,0:T(8,128)(2,1)S(1)}, bf16[4,1,64,256]{3,2,1,0:T(8,128)(2,1)S(1)}, u32[]{:S(2)}, u32[]{:S(2)}) %collective-permute-start.3) | collective-permute-done | bytes 131104 | tf_op jit(solution)/shard_map/ppermute | solution.py:15
  22.8 0.8 fusion.8
  23.5 3.1 %fusion.270 = (bf16[2,8,64,256]{3,2,1,0:T(8,128)(2,1)S(1)}, bf16[2,8,64,256]{3,2,1,0:T(8,128)(2,1)S(1)}, bf16[2,8,64,256]{3,2,1,0:T(8,128)(2,1)S(1)}, bf16[2,8,6...) fusion(bf16[4,10,66,256]{3,2,1,0:T(8,128)(2,1)S(1)} %fusion.8), kind=kLoop, calls=%fused_computation.336 | loop fusion | bytes 18874368 | tf_op jit(solution)/shard_map/slice | solution.py:30
  33.5 1.3 %fusion.184 = f32[1024,256]{1,0:T(8,128)} fusion(bf16[1024,256]{1,0:T(8,128)(2,1)S(1)} %bitcast.466, bf16[3,3,3,256,256]{4,3,2,1,0:T(8,128)(2,1)S(1)} %copy-done.3), kind=kOutput, calls=%fused_computation.245 | convolution fusion | flops 134217728 | bytes 1703936 | tf_op jit(solution)/shard_map/dot_general | solution.py:36
  34.8 2.6 %fusion.40 = bf16[1024,256]{1,0:T(8,128)(2,1)S(1)} fusion(f32[1024,256]{1,0:T(8,128)S(1)} %fusion.135, f32[1024,256]{1,0:T(8,128)S(1)} %fusion.137, f32[1024,256]{1,0:T(8,128)S(1)} %fusion.139, f32[1024,256]{1,0:T(8,128)S(1)} %fusion.141, f32[1024,256]{1,0:T(8,128)S(1)} %fusion.143, f32[1024,256]{1,0:T(8,128)S(1)} %fusion.145, ...), kind=kOutput, calls=%fused_computation.59 | convolution fusion | flops 141557760 | bytes 28442624 | tf_op jit(solution)/shard_map/dot_general | solution.py:36
  37.5 4.5 %collective-permute-start.4 = (bf16[1,8,64,256]{3,2,1,0:T(8,128)(2,1)S(1)}, bf16[1,8,64,256]{3,2,1,0:T(8,128)(2,1)S(1)}, u32[]{:S(2)}, u32[]{:S(2)}) collective-permute-start(bf16[1,8,64,256]{3,2,1,0:T(8,128)(2,1)S(1)} %bitcast.513), channel_id=1, source_target_pairs={{0,2},{2,4},{4,6},{6,8},{8,10},{10,12},{12,14},{14,16},{16,18},{18... | collective-permute-start | bytes 786440 | tf_op jit(solution)/shard_map/ppermute | solution.py:12
  42.0 1.9 %collective-permute-start.5 = (bf16[1,8,64,256]{3,2,1,0:T(8,128)(2,1)S(1)}, bf16[1,8,64,256]{3,2,1,0:T(8,128)(2,1)S(1)}, u32[]{:S(2)}, u32[]{:S(2)}) collective-permute-start(bf16[1,8,64,256]{3,2,1,0:T(8,128)(2,1)S(1)} %bitcast.512), channel_id=1, source_target_pairs={{2,0},{4,2},{6,4},{8,6},{10,8},{12,10},{14,12},{16,14},{18,16},{20... | collective-permute-start | bytes 786440 | tf_op jit(solution)/shard_map/ppermute | solution.py:15
  43.9 1.2 %fusion.109 = f32[1024,256]{1,0:T(8,128)S(1)} fusion(bf16[1024,256]{1,0:T(8,128)(2,1)S(1)} %fusion.40, bf16[3,3,3,256,256]{4,3,2,1,0:T(8,128)(2,1)} %param.7), kind=kOutput, calls=%fused_computation.170 | convolution fusion | flops 134217728 | bytes 1703936 | tf_op jit(solution)/shard_map/dot_general | solution.py:36
  45.3 5.3 %collective-permute-done.5 = bf16[1,8,64,256]{3,2,1,0:T(8,128)(2,1)S(1)} collective-permute-done((bf16[1,8,64,256]{3,2,1,0:T(8,128)(2,1)S(1)}, bf16[1,8,64,256]{3,2,1,0:T(8,128)(2,1)S(1)}, u32[]{:S(2)}, u32[]{:S(2)}) %collective-permute-start.5) | collective-permute-done | bytes 262176 | tf_op jit(solution)/shard_map/ppermute | solution.py:15
  51.0 1.3 %collective-permute-start.6 = (bf16[4,1,64,256]{3,2,1,0:T(8,128)(2,1)S(1)}, bf16[4,1,64,256]{3,2,1,0:T(8,128)(2,1)S(1)}, u32[]{:S(2)}, u32[]{:S(2)}) collective-permute-start(bf16[4,1,64,256]{3,2,1,0:T(8,128)(2,1)S(1)} %get-tuple-element.55), channel_id=1, source_target_pairs={{0,1},{2,3},{4,5},{6,7},{8,9},{10,11},{12,13},{14,15},{16,17},{18,... | collective-permute-start | bytes 393224 | tf_op jit(solution)/shard_map/ppermute | solution.py:12
  52.3 1.5 %collective-permute-start.7 = (bf16[4,1,64,256]{3,2,1,0:T(8,128)(2,1)S(1)}, bf16[4,1,64,256]{3,2,1,0:T(8,128)(2,1)S(1)}, u32[]{:S(2)}, u32[]{:S(2)}) collective-permute-start(bf16[4,1,64,256]{3,2,1,0:T(8,128)(2,1)S(1)} %get-tuple-element.56), channel_id=1, source_target_pairs={{1,0},{3,2},{5,4},{7,6},{9,8},{11,10},{13,12},{15,14},{17,16},{19,... | collective-permute-start | bytes 393224 | tf_op jit(solution)/shard_map/ppermute | solution.py:15
  54.3 3.8 %collective-permute-done.7 = bf16[4,1,64,256]{3,2,1,0:T(8,128)(2,1)S(1)} collective-permute-done((bf16[4,1,64,256]{3,2,1,0:T(8,128)(2,1)S(1)}, bf16[4,1,64,256]{3,2,1,0:T(8,128)(2,1)S(1)}, u32[]{:S(2)}, u32[]{:S(2)}) %collective-permute-start.7) | collective-permute-done | bytes 131104 | tf_op jit(solution)/shard_map/ppermute | solution.py:15
  58.1 0.8 select_maximum_fusion
  58.9 3.3 %fusion.269 = (bf16[2,8,64,256]{3,2,1,0:T(8,128)(2,1)S(1)}, bf16[2,8,64,256]{3,2,1,0:T(8,128)(2,1)S(1)}, bf16[2,8,64,256]{3,2,1,0:T(8,128)(2,1)S(1)}, bf16[2,8,6...) fusion(bf16[4,10,66,256]{3,2,1,0:T(8,128)(2,1)S(1)} %select_max, ...), kind=kLoop, calls=%fused_computation.335 | loop fusion | bytes 18874368 | tf_op jit(solution)/shard_map/slice | solution.py:30
  68.1 0.8 fusion.24
  70.7 0.6 reshape.411
  71.3 0.5 reduce_sum.9
  71.9 4.0 %all-gather = bf16[8,32,256]{2,1,0:T(8,128)(2,1)S(1)} all-gather(bf16[4,32,256]{2,1,0:T(8,128)(2,1)S(1)} %multiply_convert_fusion), channel_id=2, replica_groups=mesh['brick'=16,'chan'=2] {'chan'}, dimensions={0}, use_global_device_ids=true | all-gather | bytes 196608 | tf_op jit(solution)/shard_map/all_gather | solution.py:56
  75.9 5.4 %collective-permute-start.8 = (bf16[1,8,32,256]{3,2,1,0:T(8,128)(2,1)S(1)}, bf16[1,8,32,256]{3,2,1,0:T(8,128)(2,1)S(1)}, u32[]{:S(2)}, u32[]{:S(2)}) collective-permute-start(bf16[1,8,32,256]{3,2,1,0:T(8,128)(2,1)S(1)} %bitcast.479), channel_id=1, source_target_pairs={{0,2},{2,4},{4,6},{6,8},{8,10},{10,12},{12,14},{14,16},{16,18},{18... | collective-permute-start | bytes 393224 | tf_op jit(solution)/shard_map/ppermute | solution.py:12
  81.3 1.9 %collective-permute-start.9 = (bf16[1,8,32,256]{3,2,1,0:T(8,128)(2,1)S(1)}, bf16[1,8,32,256]{3,2,1,0:T(8,128)(2,1)S(1)}, u32[]{:S(2)}, u32[]{:S(2)}) collective-permute-start(bf16[1,8,32,256]{3,2,1,0:T(8,128)(2,1)S(1)} %bitcast.480), channel_id=1, source_target_pairs={{2,0},{4,2},{6,4},{8,6},{10,8},{12,10},{14,12},{16,14},{18,16},{20... | collective-permute-start | bytes 393224 | tf_op jit(solution)/shard_map/ppermute | solution.py:15
  83.2 5.2 %collective-permute-done.9 = bf16[1,8,32,256]{3,2,1,0:T(8,128)(2,1)S(1)} collective-permute-done((bf16[1,8,32,256]{3,2,1,0:T(8,128)(2,1)S(1)}, bf16[1,8,32,256]{3,2,1,0:T(8,128)(2,1)S(1)}, u32[]{:S(2)}, u32[]{:S(2)}) %collective-permute-start.9) | collective-permute-done | bytes 131104 | tf_op jit(solution)/shard_map/ppermute | solution.py:15
  94.3 0.8 fusion.47
  95.1 3.4 %all-to-all-start = ((bf16[1,8,32,256]{3,2,0,1:T(8,128)(2,1)}), bf16[1,8,32,256]{3,2,0,1:T(8,128)(2,1)S(1)}, u32[]{:S(2)}, u32[]{:S(2)}) async-start(bf16[1,8,32,256]{3,2,0,1:T(8,128)(2,1)} %bitcast.167), calls=%async_computation | async-start | bytes 262144 | tf_op jit(solution)/shard_map/all_to_all | solution.py:60
  98.5 4.7 %all_gather.7 = bf16[512,256]{1,0:T(8,128)(2,1)S(1)} all-gather(bf16[256,256]{1,0:T(8,128)(2,1)S(1)} %copy-done.4), channel_id=1, replica_groups=mesh['brick'=16,'chan'=2] {'chan'}, dimensions={0}, use_global_device_ids=true | all-gather | bytes 393216 | tf_op jit(solution)/shard_map/all_gather | solution.py:61
  104.3 0.9 add_convert_fusion
  (111 shorter events, 22.9 us)
Async XLA Ops:
  0.0 13.7 %copy-start = (bf16[2,8,64,256]{3,2,1,0:T(8,128)(2,1)S(1)}, bf16[2,8,64,256]{3,2,1,0:T(8,128)(2,1)}, u32[]{:S(2)}) copy-start(bf16[2,8,64,256]{3,2,1,0:T(8,128)(2,1)} %param.5) | copy-start | bytes 1572868
  0.0 18.3 %copy-start.3 = (bf16[3,3,3,256,256]{4,3,2,1,0:T(8,128)(2,1)S(1)}, bf16[3,3,3,256,256]{4,3,2,1,0:T(8,128)(2,1)}, u32[]{:S(2)}) copy-start(bf16[3,3,3,256,256]{4,3,2,1,0:T(8,128)(2,1)} %param.6) | copy-start | bytes 10616836
  1.2 7.1 %collective-permute-start = (bf16[1,8,64,256]{3,2,1,0:T(8,128)(2,1)S(1)}, bf16[1,8,64,256]{3,2,1,0:T(8,128)(2,1)S(1)}, u32[]{:S(2)}, u32[]{:S(2)}) collective-permute-start(bf16[1,8,64,256]{3,2,1,0:T(8,128)(2,1)S(1)} %get-tuple-element.94), channel_id=1, source_target_pairs={{0,2},{2,4},{4,6},{6,8},{8,10},{10,12},{12,14},{14,16},{16,18},{18... | collective-permute-start | bytes 786440 | tf_op jit(solution)/shard_map/ppermute | solution.py:12
  5.1 8.6 %collective-permute-start.1 = (bf16[1,8,64,256]{3,2,1,0:T(8,128)(2,1)S(1)}, bf16[1,8,64,256]{3,2,1,0:T(8,128)(2,1)S(1)}, u32[]{:S(2)}, u32[]{:S(2)}) collective-permute-start(bf16[1,8,64,256]{3,2,1,0:T(8,128)(2,1)S(1)} %get-tuple-element.93), channel_id=1, source_target_pairs={{2,0},{4,2},{6,4},{8,6},{10,8},{12,10},{14,12},{16,14},{18,16},{20... | collective-permute-start | bytes 786440 | tf_op jit(solution)/shard_map/ppermute | solution.py:15
  13.9 5.1 %collective-permute-start.2 = (bf16[4,1,64,256]{3,2,1,0:T(8,128)(2,1)S(1)}, bf16[4,1,64,256]{3,2,1,0:T(8,128)(2,1)S(1)}, u32[]{:S(2)}, u32[]{:S(2)}) collective-permute-start(bf16[4,1,64,256]{3,2,1,0:T(8,128)(2,1)S(1)} %get-tuple-element.60), channel_id=1, source_target_pairs={{0,1},{2,3},{4,5},{6,7},{8,9},{10,11},{12,13},{14,15},{16,17},{18,... | collective-permute-start | bytes 393224 | tf_op jit(solution)/shard_map/ppermute | solution.py:12
  17.0 5.7 %collective-permute-start.3 = (bf16[4,1,64,256]{3,2,1,0:T(8,128)(2,1)S(1)}, bf16[4,1,64,256]{3,2,1,0:T(8,128)(2,1)S(1)}, u32[]{:S(2)}, u32[]{:S(2)}) collective-permute-start(bf16[4,1,64,256]{3,2,1,0:T(8,128)(2,1)S(1)} %get-tuple-element.61), channel_id=1, source_target_pairs={{1,0},{3,2},{5,4},{7,6},{9,8},{11,10},{13,12},{15,14},{17,16},{19,... | collective-permute-start | bytes 393224 | tf_op jit(solution)/shard_map/ppermute | solution.py:15
  37.4 13.3 %copy-start.1 = (bf16[3,3,3,256,256]{4,3,2,1,0:T(8,128)(2,1)S(1)}, bf16[3,3,3,256,256]{4,3,2,1,0:T(8,128)(2,1)}, u32[]{:S(2)}) copy-start(bf16[3,3,3,256,256]{4,3,2,1,0:T(8,128)(2,1)} %param.7) | copy-start | bytes 10616836
  37.5 7.8 %collective-permute-start.4 = (bf16[1,8,64,256]{3,2,1,0:T(8,128)(2,1)S(1)}, bf16[1,8,64,256]{3,2,1,0:T(8,128)(2,1)S(1)}, u32[]{:S(2)}, u32[]{:S(2)}) collective-permute-start(bf16[1,8,64,256]{3,2,1,0:T(8,128)(2,1)S(1)} %bitcast.513), channel_id=1, source_target_pairs={{0,2},{2,4},{4,6},{6,8},{8,10},{10,12},{12,14},{14,16},{16,18},{18... | collective-permute-start | bytes 786440 | tf_op jit(solution)/shard_map/ppermute | solution.py:12
  42.0 8.6 %collective-permute-start.5 = (bf16[1,8,64,256]{3,2,1,0:T(8,128)(2,1)S(1)}, bf16[1,8,64,256]{3,2,1,0:T(8,128)(2,1)S(1)}, u32[]{:S(2)}, u32[]{:S(2)}) collective-permute-start(bf16[1,8,64,256]{3,2,1,0:T(8,128)(2,1)S(1)} %bitcast.512), channel_id=1, source_target_pairs={{2,0},{4,2},{6,4},{8,6},{10,8},{12,10},{14,12},{16,14},{18,16},{20... | collective-permute-start | bytes 786440 | tf_op jit(solution)/shard_map/ppermute | solution.py:15
  51.0 3.2 %collective-permute-start.6 = (bf16[4,1,64,256]{3,2,1,0:T(8,128)(2,1)S(1)}, bf16[4,1,64,256]{3,2,1,0:T(8,128)(2,1)S(1)}, u32[]{:S(2)}, u32[]{:S(2)}) collective-permute-start(bf16[4,1,64,256]{3,2,1,0:T(8,128)(2,1)S(1)} %get-tuple-element.55), channel_id=1, source_target_pairs={{0,1},{2,3},{4,5},{6,7},{8,9},{10,11},{12,13},{14,15},{16,17},{18,... | collective-permute-start | bytes 393224 | tf_op jit(solution)/shard_map/ppermute | solution.py:12
  52.3 5.7 %collective-permute-start.7 = (bf16[4,1,64,256]{3,2,1,0:T(8,128)(2,1)S(1)}, bf16[4,1,64,256]{3,2,1,0:T(8,128)(2,1)S(1)}, u32[]{:S(2)}, u32[]{:S(2)}) collective-permute-start(bf16[4,1,64,256]{3,2,1,0:T(8,128)(2,1)S(1)} %get-tuple-element.56), channel_id=1, source_target_pairs={{1,0},{3,2},{5,4},{7,6},{9,8},{11,10},{13,12},{15,14},{17,16},{19,... | collective-permute-start | bytes 393224 | tf_op jit(solution)/shard_map/ppermute | solution.py:15
  75.9 13.3 %copy-start.2 = (bf16[3,3,3,256,256]{4,3,2,1,0:T(8,128)(2,1)S(1)}, bf16[3,3,3,256,256]{4,3,2,1,0:T(8,128)(2,1)}, u32[]{:S(2)}) copy-start(bf16[3,3,3,256,256]{4,3,2,1,0:T(8,128)(2,1)} %param.8) | copy-start | bytes 10616836
  75.9 7.3 %collective-permute-start.8 = (bf16[1,8,32,256]{3,2,1,0:T(8,128)(2,1)S(1)}, bf16[1,8,32,256]{3,2,1,0:T(8,128)(2,1)S(1)}, u32[]{:S(2)}, u32[]{:S(2)}) collective-permute-start(bf16[1,8,32,256]{3,2,1,0:T(8,128)(2,1)S(1)} %bitcast.479), channel_id=1, source_target_pairs={{0,2},{2,4},{4,6},{6,8},{8,10},{10,12},{12,14},{14,16},{16,18},{18... | collective-permute-start | bytes 393224 | tf_op jit(solution)/shard_map/ppermute | solution.py:12
  81.3 7.2 %collective-permute-start.9 = (bf16[1,8,32,256]{3,2,1,0:T(8,128)(2,1)S(1)}, bf16[1,8,32,256]{3,2,1,0:T(8,128)(2,1)S(1)}, u32[]{:S(2)}, u32[]{:S(2)}) collective-permute-start(bf16[1,8,32,256]{3,2,1,0:T(8,128)(2,1)S(1)} %bitcast.480), channel_id=1, source_target_pairs={{2,0},{4,2},{6,4},{8,6},{10,8},{12,10},{14,12},{16,14},{18,16},{20... | collective-permute-start | bytes 393224 | tf_op jit(solution)/shard_map/ppermute | solution.py:15
  92.9 5.6 %copy-start.4 = (bf16[256,256]{1,0:T(8,128)(2,1)S(1)}, bf16[256,256]{1,0:T(8,128)(2,1)}, u32[]{:S(2)}) copy-start(bf16[256,256]{1,0:T(8,128)(2,1)} %param.9) | copy-start | bytes 393220
  95.1 8.1 %all-to-all-start = ((bf16[1,8,32,256]{3,2,0,1:T(8,128)(2,1)}), bf16[1,8,32,256]{3,2,0,1:T(8,128)(2,1)S(1)}, u32[]{:S(2)}, u32[]{:S(2)}) async-start(bf16[1,8,32,256]{3,2,0,1:T(8,128)(2,1)} %bitcast.167), calls=%async_computation | async-start | bytes 262144 | tf_op jit(solution)/shard_map/all_to_all | solution.py:60
where the time goes:
time: 106 us; the launch traced here: 105 us
  starting transfers between devices  30 us (28%)
  matrix products  27.9 us (26%)
  waiting for transfers between devices  23.7 us (22%)
  local copies, waits for them, and re-layouts  10.1 us (10%)
  blocking collectives  8.73 us (8%)
  other arithmetic  4.03 us (4%)
    dot_general x81, matrix products, convolve(): jnp.dot(window, weight[offset_x, offset_y, offset_z], preferred_element_t...  27.7 us
    ppermute x5, waiting for transfers between devices, extended(): lax.ppermute(lax.slice_in_dim(block, 0, width, axis=dim), axis, backward)  23.4 us
    ppermute x5, starting transfers between devices, extended(): lax.ppermute(lax.slice_in_dim(block, block.shape[dim] - width, None, axis...  18.1 us
    ppermute x5, starting transfers between devices, extended(): lax.ppermute(lax.slice_in_dim(block, 0, width, axis=dim), axis, backward)  8.53 us
    slice x5, local copies, waits for them, and re-layouts, convolve(): padded[offset_x:offset_x + rows_x, offset_y:offset_y + rows_y, offset_z:o...  7.32 us
    all_gather x1, blocking collectives, shards(): whole_projection = lax.all_gather(projection, 'chan', axis=0, tiled=True)  4.7 us
    all_gather x1, blocking collectives, shards(): brick_cells = lax.all_gather(pooled, 'chan', axis=1, tiled=True)  4.03 us
    all_to_all x1, starting transfers between devices, shards(): lax.all_to_all(coarse, 'chan', split_axis=1, concat_axis=3, tiled=True)  3.38 us
  transfers between devices with their start and end apart: 11, of which 7 were waited for; matrix products, arithmetic and copies ran while one was open for 3% of the time, Pallas kernels for 0%

commit v1 on v0

--- a/solution.py
+++ b/solution.py
@@ -58,7 +58,9 @@
     padded = jnp.pad(padded, ((0, 0), (1, 1), (1, 1), (0, 0)))
     coarse = jnp.maximum(convolve(padded, coarse_weight), 0.0).astype(jnp.bfloat16)
     own_cells = lax.all_to_all(coarse, "chan", split_axis=1, concat_axis=3, tiled=True)
-    whole_projection = lax.all_gather(projection, "chan", axis=0, tiled=True)
+    whole_projection = jnp.concatenate(
+        lax.all_to_all(jnp.stack([projection] * lax.axis_size("chan")), "chan", 0, 0), axis=0
+    )
     own_shape = own_cells.shape
     lifted = jnp.dot(
         own_cells.reshape(-1, own_shape[3]), whole_projection, preferred_element_type=jnp.float32

time: 106 us -> 112 us (1.057)
  waiting for transfers between devices: 23.7 us -> 30.1 us
  blocking collectives: 8.73 us -> 4.05 us
  starting transfers between devices: 30 us -> 33.4 us
    all_gather x1 -> x0, blocking collectives: 4.7 us -> none  [shards(): whole_projection = lax.all_gather(projection, 'chan', axis=0, tiled=True)]
    all_to_all x0 -> x1, waiting for transfers between devices: none -> 3.77 us  [shards(): lax.all_to_all(jnp.stack([projection] * lax.axis_size('chan')), 'chan', 0...]
    all_to_all x0 -> x1, starting transfers between devices: none -> 3.44 us  [shards(): lax.all_to_all(jnp.stack([projection] * lax.axis_size('chan')), 'chan', 0...]
    all_to_all x1, waiting for transfers between devices: 0.01 us -> 2.58 us  [shards(): lax.all_to_all(coarse, 'chan', split_axis=1, concat_axis=3, tiled=True)]
  transfers between devices with their start and end apart: 11 -> 12, of which waited for: 7 -> 9; matrix products, arithmetic and copies ran while one was open for 3% -> 4% of each run, Pallas kernels for 0% -> 0%
where the time goes in v1:
time: 112 us; the launch traced here: 111 us
  starting transfers between devices  33.4 us (30%)
  waiting for transfers between devices  30.1 us (27%)
  matrix products  27.9 us (25%)
  local copies, waits for them, and re-layouts  10.1 us (9%)
  other arithmetic  4.76 us (4%)
  blocking collectives  4.05 us (4%)
    dot_general x81, matrix products, convolve(): jnp.dot(window, weight[offset_x, offset_y, offset_z], preferred_element_t...  27.7 us
    ppermute x5, waiting for transfers between devices, extended(): lax.ppermute(lax.slice_in_dim(block, 0, width, axis=dim), axis, backward)  23.4 us
    ppermute x5, starting transfers between devices, extended(): lax.ppermute(lax.slice_in_dim(block, block.shape[dim] - width, None, axis...  18.1 us
    ppermute x5, starting transfers between devices, extended(): lax.ppermute(lax.slice_in_dim(block, 0, width, axis=dim), axis, backward)  8.53 us
    slice x5, local copies, waits for them, and re-layouts, convolve(): padded[offset_x:offset_x + rows_x, offset_y:offset_y + rows_y, offset_z:o...  7.32 us
    all_gather x1, blocking collectives, shards(): brick_cells = lax.all_gather(pooled, 'chan', axis=1, tiled=True)  4.05 us
    all_to_all x1, waiting for transfers between devices, shards(): lax.all_to_all(jnp.stack([projection] * lax.axis_size('chan')), 'chan', 0...  3.77 us
    all_to_all x1, starting transfers between devices, shards(): lax.all_to_all(jnp.stack([projection] * lax.axis_size('chan')), 'chan', 0...  3.44 us
  transfers between devices with their start and end apart: 12, of which 9 were waited for; matrix products, arithmetic and copies ran while one was open for 4% of the time, Pallas kernels for 0%

profile of v1, /device:TPU:21, one launch (start us, length us, event | category | flops | bytes accessed | tf_op | source)
XLA Modules:
  0.0 111.0 jit_solution(3259697701947125193)
XLA Ops:
  0.0 1.2 %fusion.275 = (bf16[1,8,64,256]{3,2,1,0:T(8,128)(2,1)S(1)}, bf16[1,8,64,256]{3,2,1,0:T(8,128)(2,1)S(1)}) fusion(bf16[2,8,64,256]{3,2,1,0:T(8,128)(2,1)} %param.5), kind=kLoop, calls=%fused_computation.342 | loop fusion | bytes 1048576 | tf_op jit(solution)/shard_map/slice | solution.py:15
  1.2 3.8 %collective-permute-start = (bf16[1,8,64,256]{3,2,1,0:T(8,128)(2,1)S(1)}, bf16[1,8,64,256]{3,2,1,0:T(8,128)(2,1)S(1)}, u32[]{:S(2)}, u32[]{:S(2)}) collective-permute-start(bf16[1,8,64,256]{3,2,1,0:T(8,128)(2,1)S(1)} %get-tuple-element.94), channel_id=1, source_target_pairs={{0,2},{2,4},{4,6},{6,8},{8,10},{10,12},{12,14},{14,16},{16,18},{18... | collective-permute-start | bytes 786440 | tf_op jit(solution)/shard_map/ppermute | solution.py:12
  5.1 1.9 %collective-permute-start.1 = (bf16[1,8,64,256]{3,2,1,0:T(8,128)(2,1)S(1)}, bf16[1,8,64,256]{3,2,1,0:T(8,128)(2,1)S(1)}, u32[]{:S(2)}, u32[]{:S(2)}) collective-permute-start(bf16[1,8,64,256]{3,2,1,0:T(8,128)(2,1)S(1)} %get-tuple-element.93), channel_id=1, source_target_pairs={{2,0},{4,2},{6,4},{8,6},{10,8},{12,10},{14,12},{16,14},{18,16},{20... | collective-permute-start | bytes 786440 | tf_op jit(solution)/shard_map/ppermute | solution.py:15
  7.0 1.4 %fusion.158 = f32[1024,256]{1,0:T(8,128)S(1)} fusion(bf16[1024,256]{1,0:T(8,128)(2,1)} %bitcast.428, bf16[3,3,3,256,256]{4,3,2,1,0:T(8,128)(2,1)} %param.6), kind=kOutput, calls=%fused_computation.220 | convolution fusion | flops 134217728 | bytes 1703936 | tf_op jit(solution)/shard_map/dot_general | solution.py:36
  8.4 5.3 %collective-permute-done.1 = bf16[1,8,64,256]{3,2,1,0:T(8,128)(2,1)S(1)} collective-permute-done((bf16[1,8,64,256]{3,2,1,0:T(8,128)(2,1)S(1)}, bf16[1,8,64,256]{3,2,1,0:T(8,128)(2,1)S(1)}, u32[]{:S(2)}, u32[]{:S(2)}) %collective-permute-start.1) | collective-permute-done | bytes 262176 | tf_op jit(solution)/shard_map/ppermute | solution.py:15
  13.9 3.1 %collective-permute-start.2 = (bf16[4,1,64,256]{3,2,1,0:T(8,128)(2,1)S(1)}, bf16[4,1,64,256]{3,2,1,0:T(8,128)(2,1)S(1)}, u32[]{:S(2)}, u32[]{:S(2)}) collective-permute-start(bf16[4,1,64,256]{3,2,1,0:T(8,128)(2,1)S(1)} %get-tuple-element.60), channel_id=1, source_target_pairs={{0,1},{2,3},{4,5},{6,7},{8,9},{10,11},{12,13},{14,15},{16,17},{18,... | collective-permute-start | bytes 393224 | tf_op jit(solution)/shard_map/ppermute | solution.py:12
  17.0 1.3 %collective-permute-start.3 = (bf16[4,1,64,256]{3,2,1,0:T(8,128)(2,1)S(1)}, bf16[4,1,64,256]{3,2,1,0:T(8,128)(2,1)S(1)}, u32[]{:S(2)}, u32[]{:S(2)}) collective-permute-start(bf16[4,1,64,256]{3,2,1,0:T(8,128)(2,1)S(1)} %get-tuple-element.61), channel_id=1, source_target_pairs={{1,0},{3,2},{5,4},{7,6},{9,8},{11,10},{13,12},{15,14},{17,16},{19,... | collective-permute-start | bytes 393224 | tf_op jit(solution)/shard_map/ppermute | solution.py:15
  19.0 3.8 %collective-permute-done.3 = bf16[4,1,64,256]{3,2,1,0:T(8,128)(2,1)S(1)} collective-permute-done((bf16[4,1,64,256]{3,2,1,0:T(8,128)(2,1)S(1)}, bf16[4,1,64,256]{3,2,1,0:T(8,128)(2,1)S(1)}, u32[]{:S(2)}, u32[]{:S(2)}) %collective-permute-start.3) | collective-permute-done | bytes 131104 | tf_op jit(solution)/shard_map/ppermute | solution.py:15
  22.8 0.8 fusion.8
  23.5 3.1 %fusion.268 = (bf16[2,8,64,256]{3,2,1,0:T(8,128)(2,1)S(1)}, bf16[2,8,64,256]{3,2,1,0:T(8,128)(2,1)S(1)}, bf16[2,8,64,256]{3,2,1,0:T(8,128)(2,1)S(1)}, bf16[2,8,6...) fusion(bf16[4,10,66,256]{3,2,1,0:T(8,128)(2,1)S(1)} %fusion.8), kind=kLoop, calls=%fused_computation.335 | loop fusion | bytes 18874368 | tf_op jit(solution)/shard_map/slice | solution.py:30
  33.5 1.3 %fusion.182 = f32[1024,256]{1,0:T(8,128)} fusion(bf16[1024,256]{1,0:T(8,128)(2,1)S(1)} %bitcast.468, bf16[3,3,3,256,256]{4,3,2,1,0:T(8,128)(2,1)S(1)} %copy-done.3), kind=kOutput, calls=%fused_computation.244 | convolution fusion | flops 134217728 | bytes 1703936 | tf_op jit(solution)/shard_map/dot_general | solution.py:36
  34.8 2.6 %fusion.40 = bf16[1024,256]{1,0:T(8,128)(2,1)S(1)} fusion(f32[1024,256]{1,0:T(8,128)S(1)} %fusion.133, f32[1024,256]{1,0:T(8,128)S(1)} %fusion.135, f32[1024,256]{1,0:T(8,128)S(1)} %fusion.137, f32[1024,256]{1,0:T(8,128)S(1)} %fusion.139, f32[1024,256]{1,0:T(8,128)S(1)} %fusion.141, f32[1024,256]{1,0:T(8,128)S(1)} %fusion.143, ...), kind=kOutput, calls=%fused_computation.59 | convolution fusion | flops 141557760 | bytes 28442624 | tf_op jit(solution)/shard_map/dot_general | solution.py:36
  37.5 4.5 %collective-permute-start.4 = (bf16[1,8,64,256]{3,2,1,0:T(8,128)(2,1)S(1)}, bf16[1,8,64,256]{3,2,1,0:T(8,128)(2,1)S(1)}, u32[]{:S(2)}, u32[]{:S(2)}) collective-permute-start(bf16[1,8,64,256]{3,2,1,0:T(8,128)(2,1)S(1)} %bitcast.516), channel_id=1, source_target_pairs={{0,2},{2,4},{4,6},{6,8},{8,10},{10,12},{12,14},{14,16},{16,18},{18... | collective-permute-start | bytes 786440 | tf_op jit(solution)/shard_map/ppermute | solution.py:12
  42.0 1.9 %collective-permute-start.5 = (bf16[1,8,64,256]{3,2,1,0:T(8,128)(2,1)S(1)}, bf16[1,8,64,256]{3,2,1,0:T(8,128)(2,1)S(1)}, u32[]{:S(2)}, u32[]{:S(2)}) collective-permute-start(bf16[1,8,64,256]{3,2,1,0:T(8,128)(2,1)S(1)} %bitcast.515), channel_id=1, source_target_pairs={{2,0},{4,2},{6,4},{8,6},{10,8},{12,10},{14,12},{16,14},{18,16},{20... | collective-permute-start | bytes 786440 | tf_op jit(solution)/shard_map/ppermute | solution.py:15
  43.9 1.2 %fusion.107 = f32[1024,256]{1,0:T(8,128)S(1)} fusion(bf16[1024,256]{1,0:T(8,128)(2,1)S(1)} %fusion.40, bf16[3,3,3,256,256]{4,3,2,1,0:T(8,128)(2,1)} %param.7), kind=kOutput, calls=%fused_computation.169 | convolution fusion | flops 134217728 | bytes 1703936 | tf_op jit(solution)/shard_map/dot_general | solution.py:36
  45.3 5.3 %collective-permute-done.5 = bf16[1,8,64,256]{3,2,1,0:T(8,128)(2,1)S(1)} collective-permute-done((bf16[1,8,64,256]{3,2,1,0:T(8,128)(2,1)S(1)}, bf16[1,8,64,256]{3,2,1,0:T(8,128)(2,1)S(1)}, u32[]{:S(2)}, u32[]{:S(2)}) %collective-permute-start.5) | collective-permute-done | bytes 262176 | tf_op jit(solution)/shard_map/ppermute | solution.py:15
  51.0 1.3 %collective-permute-start.6 = (bf16[4,1,64,256]{3,2,1,0:T(8,128)(2,1)S(1)}, bf16[4,1,64,256]{3,2,1,0:T(8,128)(2,1)S(1)}, u32[]{:S(2)}, u32[]{:S(2)}) collective-permute-start(bf16[4,1,64,256]{3,2,1,0:T(8,128)(2,1)S(1)} %get-tuple-element.55), channel_id=1, source_target_pairs={{0,1},{2,3},{4,5},{6,7},{8,9},{10,11},{12,13},{14,15},{16,17},{18,... | collective-permute-start | bytes 393224 | tf_op jit(solution)/shard_map/ppermute | solution.py:12
  52.3 1.5 %collective-permute-start.7 = (bf16[4,1,64,256]{3,2,1,0:T(8,128)(2,1)S(1)}, bf16[4,1,64,256]{3,2,1,0:T(8,128)(2,1)S(1)}, u32[]{:S(2)}, u32[]{:S(2)}) collective-permute-start(bf16[4,1,64,256]{3,2,1,0:T(8,128)(2,1)S(1)} %get-tuple-element.56), channel_id=1, source_target_pairs={{1,0},{3,2},{5,4},{7,6},{9,8},{11,10},{13,12},{15,14},{17,16},{19,... | collective-permute-start | bytes 393224 | tf_op jit(solution)/shard_map/ppermute | solution.py:15
  54.3 3.8 %collective-permute-done.7 = bf16[4,1,64,256]{3,2,1,0:T(8,128)(2,1)S(1)} collective-permute-done((bf16[4,1,64,256]{3,2,1,0:T(8,128)(2,1)S(1)}, bf16[4,1,64,256]{3,2,1,0:T(8,128)(2,1)S(1)}, u32[]{:S(2)}, u32[]{:S(2)}) %collective-permute-start.7) | collective-permute-done | bytes 131104 | tf_op jit(solution)/shard_map/ppermute | solution.py:15
  58.1 0.8 select_maximum_fusion
  58.9 3.3 %fusion.267 = (bf16[2,8,64,256]{3,2,1,0:T(8,128)(2,1)S(1)}, bf16[2,8,64,256]{3,2,1,0:T(8,128)(2,1)S(1)}, bf16[2,8,64,256]{3,2,1,0:T(8,128)(2,1)S(1)}, bf16[2,8,6...) fusion(bf16[4,10,66,256]{3,2,1,0:T(8,128)(2,1)S(1)} %select_max, ...), kind=kLoop, calls=%fused_computation.334 | loop fusion | bytes 18874368 | tf_op jit(solution)/shard_map/slice | solution.py:30
  68.1 0.8 fusion.24
  71.9 4.0 %all-gather = bf16[8,32,256]{2,1,0:T(8,128)(2,1)S(1)} all-gather(bf16[4,32,256]{2,1,0:T(8,128)(2,1)S(1)} %multiply_convert_fusion), channel_id=2, replica_groups=mesh['brick'=16,'chan'=2] {'chan'}, dimensions={0}, use_global_device_ids=true | all-gather | bytes 196608 | tf_op jit(solution)/shard_map/all_gather | solution.py:56
  75.9 5.3 %collective-permute-start.8 = (bf16[1,8,32,256]{3,2,1,0:T(8,128)(2,1)S(1)}, bf16[1,8,32,256]{3,2,1,0:T(8,128)(2,1)S(1)}, u32[]{:S(2)}, u32[]{:S(2)}) collective-permute-start(bf16[1,8,32,256]{3,2,1,0:T(8,128)(2,1)S(1)} %bitcast.481), channel_id=1, source_target_pairs={{0,2},{2,4},{4,6},{6,8},{8,10},{10,12},{12,14},{14,16},{16,18},{18... | collective-permute-start | bytes 393224 | tf_op jit(solution)/shard_map/ppermute | solution.py:12
  81.3 1.9 %collective-permute-start.9 = (bf16[1,8,32,256]{3,2,1,0:T(8,128)(2,1)S(1)}, bf16[1,8,32,256]{3,2,1,0:T(8,128)(2,1)S(1)}, u32[]{:S(2)}, u32[]{:S(2)}) collective-permute-start(bf16[1,8,32,256]{3,2,1,0:T(8,128)(2,1)S(1)} %bitcast.482), channel_id=1, source_target_pairs={{2,0},{4,2},{6,4},{8,6},{10,8},{12,10},{14,12},{16,14},{18,16},{20... | collective-permute-start | bytes 393224 | tf_op jit(solution)/shard_map/ppermute | solution.py:15
  83.2 5.2 %collective-permute-done.9 = bf16[1,8,32,256]{3,2,1,0:T(8,128)(2,1)S(1)} collective-permute-done((bf16[1,8,32,256]{3,2,1,0:T(8,128)(2,1)S(1)}, bf16[1,8,32,256]{3,2,1,0:T(8,128)(2,1)S(1)}, u32[]{:S(2)}, u32[]{:S(2)}) %collective-permute-start.9) | collective-permute-done | bytes 131104 | tf_op jit(solution)/shard_map/ppermute | solution.py:15
  94.3 0.8 fusion.47
  95.1 3.4 %all-to-all-start = ((bf16[1,8,32,256]{3,2,0,1:T(8,128)(2,1)}), bf16[1,8,32,256]{3,2,0,1:T(8,128)(2,1)S(1)}, u32[]{:S(2)}, u32[]{:S(2)}) async-start(bf16[1,8,32,256]{3,2,0,1:T(8,128)(2,1)} %bitcast.167), calls=%async_computation | async-start | bytes 262144 | tf_op jit(solution)/shard_map/all_to_all | solution.py:60
  99.3 2.6 %all-to-all-done = bf16[1,8,32,256]{3,2,0,1:T(8,128)(2,1)S(1)} async-done(((bf16[1,8,32,256]{3,2,0,1:T(8,128)(2,1)}), bf16[1,8,32,256]{3,2,0,1:T(8,128)(2,1)S(1)}, u32[]{:S(2)}, u32[]{:S(2)}) %all-to-all-start) | async-done | bytes 131104 | tf_op jit(solution)/shard_map/all_to_all | solution.py:60
  101.8 3.4 %all-to-all-start.1 = ((bf16[2,256,256]{2,1,0:T(8,128)(2,1)}), bf16[2,256,256]{2,1,0:T(8,128)(2,1)S(1)}, u32[]{:S(2)}, u32[]{:S(2)}) async-start(bf16[2,256,256]{2,1,0:T(8,128)(2,1)} %pad_maximum_fusion.7), calls=%async_computation.1 | async-start | bytes 524288 | tf_op jit(solution)/shard_map/all_to_all | solution.py:62
  105.5 3.8 %all-to-all-done.1 = bf16[2,256,256]{2,1,0:T(8,128)(2,1)S(1)} async-done(((bf16[2,256,256]{2,1,0:T(8,128)(2,1)}), bf16[2,256,256]{2,1,0:T(8,128)(2,1)S(1)}, u32[]{:S(2)}, u32[]{:S(2)}) %all-to-all-start.1) | async-done | bytes 262176 | tf_op jit(solution)/shard_map/all_to_all | solution.py:62
  110.1 0.9 add_convert_fusion
  (113 shorter events, 24.9 us)
Async XLA Ops:
  0.0 13.7 %copy-start = (bf16[2,8,64,256]{3,2,1,0:T(8,128)(2,1)S(1)}, bf16[2,8,64,256]{3,2,1,0:T(8,128)(2,1)}, u32[]{:S(2)}) copy-start(bf16[2,8,64,256]{3,2,1,0:T(8,128)(2,1)} %param.5) | copy-start | bytes 1572868
  0.0 18.3 %copy-start.3 = (bf16[3,3,3,256,256]{4,3,2,1,0:T(8,128)(2,1)S(1)}, bf16[3,3,3,256,256]{4,3,2,1,0:T(8,128)(2,1)}, u32[]{:S(2)}) copy-start(bf16[3,3,3,256,256]{4,3,2,1,0:T(8,128)(2,1)} %param.6) | copy-start | bytes 10616836
  1.2 7.1 %collective-permute-start = (bf16[1,8,64,256]{3,2,1,0:T(8,128)(2,1)S(1)}, bf16[1,8,64,256]{3,2,1,0:T(8,128)(2,1)S(1)}, u32[]{:S(2)}, u32[]{:S(2)}) collective-permute-start(bf16[1,8,64,256]{3,2,1,0:T(8,128)(2,1)S(1)} %get-tuple-element.94), channel_id=1, source_target_pairs={{0,2},{2,4},{4,6},{6,8},{8,10},{10,12},{12,14},{14,16},{16,18},{18... | collective-permute-start | bytes 786440 | tf_op jit(solution)/shard_map/ppermute | solution.py:12
  5.1 8.6 %collective-permute-start.1 = (bf16[1,8,64,256]{3,2,1,0:T(8,128)(2,1)S(1)}, bf16[1,8,64,256]{3,2,1,0:T(8,128)(2,1)S(1)}, u32[]{:S(2)}, u32[]{:S(2)}) collective-permute-start(bf16[1,8,64,256]{3,2,1,0:T(8,128)(2,1)S(1)} %get-tuple-element.93), channel_id=1, source_target_pairs={{2,0},{4,2},{6,4},{8,6},{10,8},{12,10},{14,12},{16,14},{18,16},{20... | collective-permute-start | bytes 786440 | tf_op jit(solution)/shard_map/ppermute | solution.py:15
  13.9 5.1 %collective-permute-start.2 = (bf16[4,1,64,256]{3,2,1,0:T(8,128)(2,1)S(1)}, bf16[4,1,64,256]{3,2,1,0:T(8,128)(2,1)S(1)}, u32[]{:S(2)}, u32[]{:S(2)}) collective-permute-start(bf16[4,1,64,256]{3,2,1,0:T(8,128)(2,1)S(1)} %get-tuple-element.60), channel_id=1, source_target_pairs={{0,1},{2,3},{4,5},{6,7},{8,9},{10,11},{12,13},{14,15},{16,17},{18,... | collective-permute-start | bytes 393224 | tf_op jit(solution)/shard_map/ppermute | solution.py:12
  17.0 5.7 %collective-permute-start.3 = (bf16[4,1,64,256]{3,2,1,0:T(8,128)(2,1)S(1)}, bf16[4,1,64,256]{3,2,1,0:T(8,128)(2,1)S(1)}, u32[]{:S(2)}, u32[]{:S(2)}) collective-permute-start(bf16[4,1,64,256]{3,2,1,0:T(8,128)(2,1)S(1)} %get-tuple-element.61), channel_id=1, source_target_pairs={{1,0},{3,2},{5,4},{7,6},{9,8},{11,10},{13,12},{15,14},{17,16},{19,... | collective-permute-start | bytes 393224 | tf_op jit(solution)/shard_map/ppermute | solution.py:15
  37.4 13.3 %copy-start.1 = (bf16[3,3,3,256,256]{4,3,2,1,0:T(8,128)(2,1)S(1)}, bf16[3,3,3,256,256]{4,3,2,1,0:T(8,128)(2,1)}, u32[]{:S(2)}) copy-start(bf16[3,3,3,256,256]{4,3,2,1,0:T(8,128)(2,1)} %param.7) | copy-start | bytes 10616836
  37.5 7.8 %collective-permute-start.4 = (bf16[1,8,64,256]{3,2,1,0:T(8,128)(2,1)S(1)}, bf16[1,8,64,256]{3,2,1,0:T(8,128)(2,1)S(1)}, u32[]{:S(2)}, u32[]{:S(2)}) collective-permute-start(bf16[1,8,64,256]{3,2,1,0:T(8,128)(2,1)S(1)} %bitcast.516), channel_id=1, source_target_pairs={{0,2},{2,4},{4,6},{6,8},{8,10},{10,12},{12,14},{14,16},{16,18},{18... | collective-permute-start | bytes 786440 | tf_op jit(solution)/shard_map/ppermute | solution.py:12
  42.0 8.6 %collective-permute-start.5 = (bf16[1,8,64,256]{3,2,1,0:T(8,128)(2,1)S(1)}, bf16[1,8,64,256]{3,2,1,0:T(8,128)(2,1)S(1)}, u32[]{:S(2)}, u32[]{:S(2)}) collective-permute-start(bf16[1,8,64,256]{3,2,1,0:T(8,128)(2,1)S(1)} %bitcast.515), channel_id=1, source_target_pairs={{2,0},{4,2},{6,4},{8,6},{10,8},{12,10},{14,12},{16,14},{18,16},{20... | collective-permute-start | bytes 786440 | tf_op jit(solution)/shard_map/ppermute | solution.py:15
  51.0 3.2 %collective-permute-start.6 = (bf16[4,1,64,256]{3,2,1,0:T(8,128)(2,1)S(1)}, bf16[4,1,64,256]{3,2,1,0:T(8,128)(2,1)S(1)}, u32[]{:S(2)}, u32[]{:S(2)}) collective-permute-start(bf16[4,1,64,256]{3,2,1,0:T(8,128)(2,1)S(1)} %get-tuple-element.55), channel_id=1, source_target_pairs={{0,1},{2,3},{4,5},{6,7},{8,9},{10,11},{12,13},{14,15},{16,17},{18,... | collective-permute-start | bytes 393224 | tf_op jit(solution)/shard_map/ppermute | solution.py:12
  52.3 5.7 %collective-permute-start.7 = (bf16[4,1,64,256]{3,2,1,0:T(8,128)(2,1)S(1)}, bf16[4,1,64,256]{3,2,1,0:T(8,128)(2,1)S(1)}, u32[]{:S(2)}, u32[]{:S(2)}) collective-permute-start(bf16[4,1,64,256]{3,2,1,0:T(8,128)(2,1)S(1)} %get-tuple-element.56), channel_id=1, source_target_pairs={{1,0},{3,2},{5,4},{7,6},{9,8},{11,10},{13,12},{15,14},{17,16},{19,... | collective-permute-start | bytes 393224 | tf_op jit(solution)/shard_map/ppermute | solution.py:15
  75.9 13.3 %copy-start.2 = (bf16[3,3,3,256,256]{4,3,2,1,0:T(8,128)(2,1)S(1)}, bf16[3,3,3,256,256]{4,3,2,1,0:T(8,128)(2,1)}, u32[]{:S(2)}) copy-start(bf16[3,3,3,256,256]{4,3,2,1,0:T(8,128)(2,1)} %param.8) | copy-start | bytes 10616836
  75.9 7.3 %collective-permute-start.8 = (bf16[1,8,32,256]{3,2,1,0:T(8,128)(2,1)S(1)}, bf16[1,8,32,256]{3,2,1,0:T(8,128)(2,1)S(1)}, u32[]{:S(2)}, u32[]{:S(2)}) collective-permute-start(bf16[1,8,32,256]{3,2,1,0:T(8,128)(2,1)S(1)} %bitcast.481), channel_id=1, source_target_pairs={{0,2},{2,4},{4,6},{6,8},{8,10},{10,12},{12,14},{14,16},{16,18},{18... | collective-permute-start | bytes 393224 | tf_op jit(solution)/shard_map/ppermute | solution.py:12
  81.3 7.2 %collective-permute-start.9 = (bf16[1,8,32,256]{3,2,1,0:T(8,128)(2,1)S(1)}, bf16[1,8,32,256]{3,2,1,0:T(8,128)(2,1)S(1)}, u32[]{:S(2)}, u32[]{:S(2)}) collective-permute-start(bf16[1,8,32,256]{3,2,1,0:T(8,128)(2,1)S(1)} %bitcast.482), channel_id=1, source_target_pairs={{2,0},{4,2},{6,4},{8,6},{10,8},{12,10},{14,12},{16,14},{18,16},{20... | collective-permute-start | bytes 393224 | tf_op jit(solution)/shard_map/ppermute | solution.py:15
  92.9 5.6 %copy-start.4 = (bf16[256,256]{1,0:T(8,128)(2,1)S(1)}, bf16[256,256]{1,0:T(8,128)(2,1)}, u32[]{:S(2)}) copy-start(bf16[256,256]{1,0:T(8,128)(2,1)} %param.9) | copy-start | bytes 393220
  95.1 6.7 %all-to-all-start = ((bf16[1,8,32,256]{3,2,0,1:T(8,128)(2,1)}), bf16[1,8,32,256]{3,2,0,1:T(8,128)(2,1)S(1)}, u32[]{:S(2)}, u32[]{:S(2)}) async-start(bf16[1,8,32,256]{3,2,0,1:T(8,128)(2,1)} %bitcast.167), calls=%async_computation | async-start | bytes 262144 | tf_op jit(solution)/shard_map/all_to_all | solution.py:60
  101.8 7.5 %all-to-all-start.1 = ((bf16[2,256,256]{2,1,0:T(8,128)(2,1)}), bf16[2,256,256]{2,1,0:T(8,128)(2,1)S(1)}, u32[]{:S(2)}, u32[]{:S(2)}) async-start(bf16[2,256,256]{2,1,0:T(8,128)(2,1)} %pad_maximum_fusion.7), calls=%async_computation.1 | async-start | bytes 524288 | tf_op jit(solution)/shard_map/all_to_all | solution.py:62
